TPU v7x, 32 devices: a whole 2x2x4 slice. The times are simulated.
32 devices in a mesh: groups: 2 (over y), head: 4 (over z), state: 4 (over x, core).
Axes of the slice: x: 2, y: 2, z: 4, core: 2. Of those that a mesh axis runs over, the one named last changes fastest.
Arguments:
- tokens: bfloat16 [32, 2048], P(('groups', 'head'), 'state'), parts along dimension 0, may hold values from -20 to 20
- mixer_norm: float32 [2048], P('state'), may hold values from 0.1 to 1.9
- input_proj: bfloat16 [2, 2048, 8192], P(None, 'state', 'head'), may hold values from -0.125 to 0.125
- conv_weight: float32 [4, 8192], P(None, 'head'), may hold values from -3 to 3
- conv_bias: float32 [8192], P('head'), may hold values from -3 to 3
- conv_state: float32 [3, 32, 8192], P(None, 'groups', 'head'), parts along dimension 1, may hold values from -6 to 6
- state_proj: bfloat16 [8192, 288], P('head'), may hold values from -0.125 to 0.125
- step_gain: float32 [256], replicated, may hold values from 0.1 to 1.9
- step_proj: bfloat16 [256, 8192], P(None, 'head'), may hold values from -0.375 to 0.375
- step_bias: float32 [8192], P('head'), may hold values from -6 to -1
- decay_log: float32 [16, 8192], P('state', 'head'), may hold values from 0 to 2.77
- skip_gain: float32 [8192], P('head'), may hold values from 0.5 to 1.5
- ssm_state: float32 [16, 32, 8192], P('state', 'groups', 'head'), parts along dimension 1, may hold values from -6 to 6
- output_proj: bfloat16 [8192, 2048], P('head', 'state'), may hold values from -0.0625 to 0.0625
- moe_norm: float32 [2048], replicated, may hold values from 0.1 to 1.9
- router_weight: float32 [2048, 8], replicated, may hold values from -0.125 to 0.125
- expert_ids: int32 [32, 2], P(('groups', 'head')), parts along dimension 0, may hold values from 0 to 7, as said below
- slot_ids: int32 [32, 2], P(('groups', 'head')), parts along dimension 0, may hold values from 0 to 3, as said below
- gate_proj: bfloat16 [8, 2048, 7168], P('head', None, 'state'), may hold values from -0.125 to 0.125
- up_proj: bfloat16 [8, 2048, 7168], P('head', None, 'state'), may hold values from -0.125 to 0.125
- down_proj: bfloat16 [8, 7168, 2048], P('head', 'state'), may hold values from -0.0625 to 0.0625
Outputs:
- layer_out: bfloat16 [32, 2048], P(('groups', 'head'), 'state'), parts along dimension 0
- new_conv: float32 [3, 32, 8192], P(None, 'groups', 'head'), parts along dimension 1
- new_state: float32 [16, 32, 8192], P('state', 'groups', 'head'), parts along dimension 1
- expert_load: float32 [16], P('groups'), parts along dimension 0
- aux_loss: float32 [2], P('groups'), parts along dimension 0
There are 2 independent parts, one for each index of `groups`. A program takes and returns all parts, laid end to end along the dimension named above; an argument that names none is the same for every part. Nothing has to cross between parts.
Inputs may be any that keep to these rules, and one draw needn't show every extreme that they name: `expert_ids`: each row names 2 different experts. One expert, the same on every device, is named by every row. `slot_ids`: among the choices of one aligned block of 4 rows that name one expert, the slot positions are distinct and run from 0 to their count less one.
All inputs are finite; a program needn't handle non-finite values.
Results may differ from a plain program's by a relative error of at most 0.007.
Values may be sent and summed in bfloat16 or wider, within the bound.
A program may use at most 128 MiB of HBM per device.

v0:
```python
import jax
import jax.numpy as jnp
from jax import lax
from jax.sharding import PartitionSpec as P

D = 2048
D_STATE = 16
DT_RANK = 256
EXPERTS = 8
TOPK = 2
CAP = 2
NORM_EPS = 1e-05
STEP_EPS = 1e-06


def expert_ffn(received, gate_proj, up_proj, down_proj):
    gate_val = jnp.einsum("nlcd,ldf->nlcf", received, gate_proj, preferred_element_type=jnp.float32)
    up_val = jnp.einsum("nlcd,ldf->nlcf", received, up_proj, preferred_element_type=jnp.float32)
    hidden = (jax.nn.silu(gate_val) * up_val).astype(jnp.bfloat16)
    return jnp.einsum("nlcf,lfd->nlcd", hidden, down_proj, preferred_element_type=jnp.float32)


def per_device(
    tokens,
    mixer_norm,
    input_proj,
    conv_weight,
    conv_bias,
    conv_state,
    state_proj,
    step_gain,
    step_proj,
    step_bias,
    decay_log,
    skip_gain,
    ssm_state,
    output_proj,
    moe_norm,
    router_weight,
    expert_ids,
    slot_ids,
    gate_proj,
    up_proj,
    down_proj,
):
    head_count = lax.axis_size("head")
    state_index = lax.axis_index("state")
    own_rows = tokens.shape[0]
    tok_f32 = tokens.astype(jnp.float32)
    first_sq = lax.psum(jnp.sum(tok_f32 * tok_f32, axis=1), "state")
    inv_first = lax.rsqrt(first_sq / D + NORM_EPS)[:, None]
    normed = (tok_f32 * inv_first * mixer_norm).astype(jnp.bfloat16)
    branch_part = jnp.einsum(
        "td,kdc->ktc",
        lax.all_gather(normed, "head", axis=0, tiled=True),
        input_proj,
        preferred_element_type=jnp.float32,
    )
    branch_full = lax.psum(branch_part, "state")
    conv_input = branch_full[0]
    gate_branch = branch_full[1]
    window = jnp.concatenate([conv_state, conv_input[None]], axis=0)
    conv_out = jax.nn.silu(jnp.sum(conv_weight[:, None, :] * window, axis=0) + conv_bias)
    new_conv = window[1:]
    proj_part = jnp.dot(
        conv_out.astype(jnp.bfloat16), state_proj, preferred_element_type=jnp.float32
    )
    projected = lax.psum(proj_part, "head")
    step_low = projected[:, :DT_RANK]
    state_slab = decay_log.shape[0]
    b_input = lax.dynamic_slice_in_dim(projected, DT_RANK + state_index * state_slab, state_slab, 1)
    c_output = lax.dynamic_slice_in_dim(
        projected, DT_RANK + D_STATE + state_index * state_slab, state_slab, 1
    )
    step_inv = lax.rsqrt(jnp.mean(step_low * step_low, axis=1, keepdims=True) + STEP_EPS)
    step_normed = (step_low * step_inv * step_gain).astype(jnp.bfloat16)
    step_size = jax.nn.softplus(
        jnp.dot(step_normed, step_proj, preferred_element_type=jnp.float32) + step_bias
    )
    decay_rate = jnp.exp(-step_size[None] * jnp.exp(decay_log)[:, None, :])
    new_state = decay_rate * ssm_state + step_size[None] * b_input.T[:, :, None] * conv_out[None]
    read_part = jnp.sum(c_output.T[:, :, None] * new_state, axis=0)
    readout = lax.psum(read_part, "state")
    mixer_act = ((readout + skip_gain * conv_out) * jax.nn.silu(gate_branch)).astype(jnp.bfloat16)
    mixer_sum = lax.psum_scatter(
        jnp.dot(mixer_act, output_proj, preferred_element_type=jnp.float32),
        "head",
        scatter_dimension=0,
        tiled=True,
    )
    residual = (tok_f32 + mixer_sum).astype(jnp.bfloat16)
    full_rows = lax.all_gather(residual, "state", axis=1, tiled=True).astype(jnp.float32)
    inv_second = lax.rsqrt(jnp.mean(full_rows * full_rows, axis=1, keepdims=True) + NORM_EPS)
    scaled = full_rows * moe_norm
    logits = inv_second * jnp.dot(scaled, router_weight, precision=lax.Precision.HIGHEST)
    row_normed = (scaled * inv_second).astype(jnp.bfloat16)
    expert_hit = expert_ids[:, :, None] == jnp.arange(EXPERTS, dtype=jnp.int32)[None, None, :]
    chosen = jnp.sum(jnp.where(expert_hit, logits[:, None, :], 0.0), axis=2)
    gate_probs = jax.nn.sigmoid(chosen - chosen[:, ::-1])
    kept_mask = slot_ids < CAP
    mix_weight = jnp.where(kept_mask, gate_probs, 0.0)
    slot_hit = slot_ids[:, :, None] == jnp.arange(CAP, dtype=jnp.int32)[None, None, :]
    slot_place = expert_hit[:, :, :, None] & slot_hit[:, :, None, :]
    dispatch = jnp.sum(slot_place.astype(jnp.int32), axis=1).astype(jnp.bfloat16)
    combine_weight = jnp.sum(jnp.where(slot_place, mix_weight[:, :, None, None], 0.0), axis=1)
    outgoing = jnp.einsum(
        "tec,td->ecd", dispatch, row_normed, preferred_element_type=jnp.float32
    ).astype(jnp.bfloat16)
    row_width = outgoing.shape[2]
    local_experts = gate_proj.shape[0]
    expert_groups = EXPERTS // local_experts
    copies = head_count * local_experts // EXPERTS
    outgoing = jnp.broadcast_to(
        outgoing.reshape(expert_groups, 1, local_experts, CAP, row_width),
        (expert_groups, copies, local_experts, CAP, row_width),
    )
    outgoing = outgoing.reshape(head_count, local_experts, CAP, row_width)
    partial_out = expert_ffn(
        lax.all_to_all(outgoing, "head", split_axis=0, concat_axis=0, tiled=True),
        gate_proj,
        up_proj,
        down_proj,
    )
    returned = lax.all_to_all(
        partial_out.astype(jnp.bfloat16), "head", split_axis=0, concat_axis=0, tiled=True
    ).astype(partial_out.dtype)
    per_expert = returned.reshape(expert_groups, copies, local_experts, CAP, row_width).sum(axis=1)
    per_expert = per_expert.reshape(EXPERTS, CAP, row_width)
    expert_mix = jnp.einsum(
        "tec,ecd->td", combine_weight, per_expert, precision=lax.Precision.HIGHEST
    )
    expert_mix = lax.psum_scatter(
        expert_mix.astype(jnp.bfloat16), "state", scatter_dimension=1, tiled=True
    ).astype(jnp.float32)
    layer_out = (residual.astype(jnp.float32) + expert_mix).astype(jnp.bfloat16)
    load_own = jnp.sum(jnp.where(expert_hit & kept_mask[:, :, None], 1.0, 0.0), axis=(0, 1)).astype(
        jnp.float32
    )
    prob_own = jnp.sum(jax.nn.sigmoid(logits), axis=0)
    load_sum, prob_sum = lax.psum((load_own, prob_own), "head")
    total_rows = head_count * own_rows
    aux_value = EXPERTS * jnp.sum(load_sum / (total_rows * TOPK) * (prob_sum / total_rows))
    return (layer_out, new_conv, new_state, load_sum, aux_value.reshape(1))


def solution(mesh):
    return jax.shard_map(
        per_device,
        mesh=mesh,
        in_specs=(
            P(("groups", "head"), "state"),
            P("state"),
            P(None, "state", "head"),
            P(None, "head"),
            P("head"),
            P(None, "groups", "head"),
            P("head", None),
            P(),
            P(None, "head"),
            P("head"),
            P("state", "head"),
            P("head"),
            P("state", "groups", "head"),
            P("head", "state"),
            P(),
            P(),
            P(("groups", "head"), None),
            P(("groups", "head"), None),
            P("head", None, "state"),
            P("head", None, "state"),
            P("head", "state", None),
        ),
        out_specs=(
            P(("groups", "head"), "state"),
            P(None, "groups", "head"),
            P("state", "groups", "head"),
            P("groups"),
            P("groups"),
        ),
        check_vma=False,
    )
```

profile of v0, /device:TPU:0, one launch (start us, length us, event | category | flops | bytes accessed | tf_op | source)
XLA Modules:
  0.0 225.7 jit_solution(13633011839943154887)
XLA Ops:
  7.2 0.9 fusion.46
  8.2 8.4 %psum.42 = f32[4]{0:T(128)S(1)} all-reduce(f32[4]{0:T(128)S(1)} %fusion.46), channel_id=1, replica_groups=mesh['groups'=2,'head'=4,'state'=4] {'state'}, use_global_device_ids=true, to_apply=%region_1.0 | all-reduce | flops 4 | bytes 32 | tf_op jit(solution)/shard_map/psum | solution.py:50
  16.6 0.8 fusion.52
  17.4 13.4 %all-gather = bf16[4,4,512]{2,1,0:T(4,128)(2,1)S(1)} all-gather(bf16[1,4,512]{2,1,0:T(4,128)(2,1)S(1)} %fusion.52), channel_id=1, replica_groups=mesh['groups'=2,'head'=4,'state'=4] {'head'}, dimensions={0}, use_global_device_ids=true | all-gather | bytes 20480 | tf_op jit(solution)/shard_map/all_gather | solution.py:55
  30.8 3.6 %convolution_bitcast_fusion = f32[2,16,2048]{2,1,0:T(8,128)} fusion(bf16[16,512,1]{1,0,2:T(8,128)(2,1)S(1)} %reshape.86, bf16[2,512,2048]{2,1,0:T(8,128)(2,1)} %param.23), kind=kOutput, calls=%fused_computation.6 | convolution fusion | flops 67108864 | bytes 4472832 | tf_op jit(solution)/shard_map/td,kdc->ktc/dot_general | solution.py:53
  34.4 0.8 iota_compare_fusion
  35.2 0.7 iota_compare_fusion.1
  35.9 0.7 broadcast_compare_fusion
  36.5 0.8 exp.33
  37.3 1.2 dynamic-slice
  39.2 0.1 fusion.45
  39.3 27.6 %all-reduce.5.cloned.1.call-done = f32[2,16,2048]{2,1,0:T(8,128)} async-done(((f32[2,16,2048]{2,1,0:T(8,128)}), f32[2,16,2048]{2,1,0:T(8,128)}) %all-reduce.5.cloned.1.call-update) | async-done | bytes 262160 | tf_op jit(solution)/shard_map/psum | solution.py:59
  66.9 0.9 slice.16
  67.8 1.1 fusion.26
  68.9 0.7 divide_multiply_fusion
  69.6 1.7 fusion.31
  71.3 19.0 %psum.44 = f32[16,288]{1,0:T(8,128)S(1)} all-reduce(f32[16,288]{1,0:T(8,128)S(1)} %fusion.31), channel_id=1, replica_groups=mesh['groups'=2,'head'=4,'state'=4] {'head'}, use_global_device_ids=true, to_apply=%region_4.5 | all-reduce | flops 4608 | bytes 36864 | tf_op jit(solution)/shard_map/psum | solution.py:68
  90.3 0.1 multiply_reduce_fusion.1
  90.5 0.1 copy.53
  90.6 0.1 copy.54
  90.7 1.5 fusion.56
  92.2 2.7 %multiply_reduce_fusion = (f32[16,2048]{1,0:T(8,128)}, f32[4,16,2048]{2,1,0:T(8,128)}) fusion(f32[4,16]{1,0:T(4,128)S(1)} %copy.53, f32[16,2048]{1,0:T(8,128)S(1)} %divide_multiply_fusion, f32[4,16]{1,0:T(4,128)S(1)} %copy.54, f32[16,2048]{1,0:T(8,128)S(1)} %get-tuple-element.14, f32[4,16,2048]{2,1,0:T(8,128)} %param.33, f32[4,2048]{1,0:T(4,128)S(1)} %exp.33, ...), kind=kLoop, calls=%fused_computation.23 | loop fusion | flops 884736 | bytes 1606144 | tf_op jit(solution)/shard_map/reduce_sum | solution.py:82
  94.9 1.7 fusion.27
  96.6 27.5 %all-reduce.7.cloned.1.call-done = f32[16,2048]{1,0:T(8,128)} async-done(((f32[16,2048]{1,0:T(8,128)}), f32[16,2048]{1,0:T(8,128)}) %all-reduce.7.cloned.1.call-update) | async-done | bytes 131088 | tf_op jit(solution)/shard_map/psum | solution.py:83
  124.1 1.3 fusion.28
  125.5 19.0 %all-reduce = f32[16,512]{1,0:T(8,128)S(1)} all-reduce(f32[16,512]{1,0:T(8,128)S(1)} %fusion.28), channel_id=2, replica_groups=mesh['groups'=2,'head'=4,'state'=4] {'head'}, use_global_device_ids=true, to_apply=%region_8.9.clone | all-reduce | flops 8192 | bytes 65536
  144.5 0.7 fusion.49
  145.2 5.2 %all_gather.7 = bf16[4,2048]{1,0:T(4,128)(2,1)S(1)} all-gather(bf16[4,512]{1,0:T(4,128)(2,1)S(1)} %fusion.49), channel_id=1, replica_groups=mesh['groups'=2,'head'=4,'state'=4] {'state'}, dimensions={1}, use_global_device_ids=true | all-gather | bytes 20480 | tf_op jit(solution)/shard_map/all_gather | solution.py:92
  150.4 0.1 fusion.38
  150.5 1.1 fusion.54
  151.6 0.9 convolution_convert_fusion
  152.6 0.7 copy.63
  153.2 3.3 %all-to-all-start = ((bf16[4,2,2,2048]{3,2,1,0:T(2,128)(2,1)}), bf16[4,2,2,2048]{3,2,1,0:T(2,128)(2,1)S(1)}, u32[]{:S(2)}, u32[]{:S(2)}) async-start(bf16[4,2,2,2048]{3,2,1,0:T(2,128)(2,1)} %bitcast.6), calls=%async_computation | async-start | bytes 131072 | tf_op jit(solution)/shard_map/all_to_all | solution.py:119
  156.5 0.2 select_reduce_fusion
  156.7 12.1 %all-reduce.1 = (f32[8]{0:T(128)S(1)}, f32[8]{0:T(128)S(1)}) all-reduce(f32[8]{0:T(128)S(1)} %get-tuple-element.5, f32[8]{0:T(128)S(1)} %get-tuple-element.15), channel_id=1, replica_groups=mesh['groups'=2,'head'=4,'state'=4] {'head'}, use_global_device_ids=true, to_apply=%region_15.16 | all-reduce | flops 16 | bytes 128 | tf_op jit(solution)/shard_map/psum | solution.py:140
  168.9 7.5 %fusion.6 = f32[4,2,2,1792]{3,0,2,1:T(4,128)S(1)} fusion(bf16[2,2048,1792]{2,1,0:T(8,128)(2,1)} %param.39, bf16[4,2,2,2048]{3,2,1,0:T(2,128)(2,1)S(1)} %all-to-all-done), kind=kOutput, calls=%fused_computation.7 | convolution fusion | flops 117440512 | bytes 14860288 | tf_op jit(solution)/shard_map/nlcd,ldf->nlcf/dot_general | solution.py:17
  176.4 7.5 %fusion.15 = bf16[4,2,2,1792]{3,0,2,1:T(4,128)(2,1)S(1)} fusion(bf16[2,2048,1792]{2,1,0:T(8,128)(2,1)} %param.40, f32[4,2,2,1792]{3,0,2,1:T(4,128)S(1)} %fusion.6, bf16[4,2,2,2048]{3,2,1,0:T(2,128)(2,1)S(1)} %all-to-all-done), kind=kOutput, calls=%fused_computation.11 | convolution fusion | flops 117612544 | bytes 14917632 | tf_op jit(solution)/shard_map/nlcd,ldf->nlcf/dot_general | solution.py:18
  183.9 2.1 fusion.21
  186.0 0.7 copy.58
  186.7 3.3 %all-to-all-start.1 = ((bf16[4,2,2,2048]{3,2,1,0:T(2,128)(2,1)}), bf16[4,2,2,2048]{3,2,1,0:T(2,128)(2,1)S(1)}, u32[]{:S(2)}, u32[]{:S(2)}) async-start(bf16[4,2,2,2048]{3,2,1,0:T(2,128)(2,1)} %copy.58), calls=%async_computation.1 | async-start | bytes 131072 | tf_op jit(solution)/shard_map/all_to_all | solution.py:124
  190.1 0.1 fusion.44
  190.1 5.6 %all-to-all-done.1 = bf16[4,2,2,2048]{3,2,1,0:T(2,128)(2,1)S(1)} async-done(((bf16[4,2,2,2048]{3,2,1,0:T(2,128)(2,1)}), bf16[4,2,2,2048]{3,2,1,0:T(2,128)(2,1)S(1)}, u32[]{:S(2)}, u32[]{:S(2)}) %all-to-all-start.1) | async-done | bytes 65568 | tf_op jit(solution)/shard_map/all_to_all | solution.py:124
  195.7 0.2 fusion.24
  196.0 1.1 copy.64
  197.0 0.6 multiply_reduce_fusion.2
  198.3 18.1 %reduce-scatter.4.cloned.1.call-done = bf16[512,4]{1,0:T(8,128)(2,1)} async-done(((bf16[2048,4]{1,0:T(8,128)(2,1)}), bf16[512,4]{1,0:T(8,128)(2,1)}) %reduce-scatter.4.cloned.1.call-update) | async-done | bytes 4112
  216.4 1.0 copy.65
  217.4 0.6 add_convert_fusion
  (31 shorter events, 0.4 us)
Async XLA Ops:
  7.2 117.0 %copy-start = (bf16[2048,512]{1,0:T(8,128)(2,1)S(1)}, bf16[2048,512]{1,0:T(8,128)(2,1)}, u32[]{:S(2)}) copy-start(bf16[2048,512]{1,0:T(8,128)(2,1)} %param.34) | copy-start | bytes 6291460
  7.2 149.4 %copy-start.1 = (s32[4,2]{0,1:T(2,128)S(1)}, s32[4,2]{0,1:T(2,128)}, u32[]{:S(2)}) copy-start(s32[4,2]{0,1:T(2,128)} %param.37) | copy-start | bytes 100
  7.2 149.5 %copy-start.2 = (s32[4,2]{0,1:T(2,128)S(1)}, s32[4,2]{0,1:T(2,128)}, u32[]{:S(2)}) copy-start(s32[4,2]{0,1:T(2,128)} %param.38) | copy-start | bytes 100
  7.2 59.7 %all-reduce.5.cloned.1.call-start = ((), (), s32[]{:S(2)}) async-start(), calls=%async_computation.3 | async-start | bytes 524288 | tf_op jit(solution)/shard_map/psum | solution.py:59
  34.4 89.8 %all-reduce.7.cloned.1.call-start = ((), (), s32[]{:S(2)}) async-start(), calls=%async_computation.4 | async-start | bytes 262144 | tf_op jit(solution)/shard_map/psum | solution.py:83
  153.2 15.7 %all-to-all-start = ((bf16[4,2,2,2048]{3,2,1,0:T(2,128)(2,1)}), bf16[4,2,2,2048]{3,2,1,0:T(2,128)(2,1)S(1)}, u32[]{:S(2)}, u32[]{:S(2)}) async-start(bf16[4,2,2,2048]{3,2,1,0:T(2,128)(2,1)} %bitcast.6), calls=%async_computation | async-start | bytes 131072 | tf_op jit(solution)/shard_map/all_to_all | solution.py:119
  168.9 28.1 %copy-start.3 = (f32[8]{0:T(128)}, f32[8]{0:T(128)S(1)}, u32[]{:S(2)}) copy-start(f32[8]{0:T(128)S(1)} %get-tuple-element.7) | copy-start | bytes 100
  168.9 15.0 %slice-start = ((s8[14680064]{0:T(1024)(128)(4,1)}), s8[4194304]{0:T(1024)(128)(4,1)S(1)}, s32[]{:S(2)}) async-start(s8[14680064]{0:T(1024)(128)(4,1)} %bitcast.71), calls=%async_computation.6 | async-start | bytes 8388608
  168.9 15.0 %slice-start.1 = ((s8[14680064]{0:T(1024)(128)(4,1)}), s8[4194304]{0:T(1024)(128)(4,1)S(1)}, s32[]{:S(2)}) async-start(s8[14680064]{0:T(1024)(128)(4,1)} %bitcast.71), calls=%async_computation.7 | async-start | bytes 8388608
  176.4 7.5 %slice-start.2 = ((s8[14680064]{0:T(1024)(128)(4,1)}), s8[4194304]{0:T(1024)(128)(4,1)S(1)}, s32[]{:S(2)}) async-start(s8[14680064]{0:T(1024)(128)(4,1)} %bitcast.71), calls=%async_computation.8 | async-start | bytes 8388608
  176.4 7.5 %slice-start.3 = ((s8[14680064]{0:T(1024)(128)(4,1)}), s8[2097152]{0:T(1024)(128)(4,1)S(1)}, s32[]{:S(2)}) async-start(s8[14680064]{0:T(1024)(128)(4,1)} %bitcast.71), calls=%async_computation.9 | async-start | bytes 4194304
  186.7 9.0 %all-to-all-start.1 = ((bf16[4,2,2,2048]{3,2,1,0:T(2,128)(2,1)}), bf16[4,2,2,2048]{3,2,1,0:T(2,128)(2,1)S(1)}, u32[]{:S(2)}, u32[]{:S(2)}) async-start(bf16[4,2,2,2048]{3,2,1,0:T(2,128)(2,1)} %copy.58), calls=%async_computation.1 | async-start | bytes 131072 | tf_op jit(solution)/shard_map/all_to_all | solution.py:124
  190.0 26.4 %reduce-scatter.4.cloned.1.call-start = ((), (), s32[]{:S(2)}) async-start(), calls=%async_computation.5 | async-start | bytes 655360
Sparse Core Ops, SparseCore 0:
  34.5 32.3 all-reduce.4
  95.0 29.0 all-reduce.6
  197.2 19.2 reduce-scatter.3
where the time goes:
time: 227 us; the launch traced here: 226 us
  waiting for transfers between devices  78.8 us (35%)
  blocking collectives  77.1 us (34%)
  matrix products  27.5 us (12%)
  between operations  16.4 us (7%)
  other arithmetic  12.6 us (6%)
  local copies, waits for them, and re-layouts  6.69 us (3%)
  starting transfers between devices  6.69 us (3%)
    psum x1, waiting for transfers between devices, per_device(): branch_full = lax.psum(branch_part, 'state')  27.6 us
    psum x1, waiting for transfers between devices, per_device(): readout = lax.psum(read_part, 'state')  27.5 us
    unnamed x1, blocking collectives  19 us
    psum x1, blocking collectives, per_device(): projected = lax.psum(proj_part, 'head')  19 us
    unnamed x4, waiting for transfers between devices  18.2 us
    all_gather x1, blocking collectives, per_device(): lax.all_gather(normed, 'head', axis=0, tiled=True)  13.4 us
    psum x1, blocking collectives, per_device(): load_sum, prob_sum = lax.psum((load_own, prob_own), 'head')  12.1 us
    psum x1, blocking collectives, per_device(): first_sq = lax.psum(jnp.sum(tok_f32 * tok_f32, axis=1), 'state')  8.36 us
  transfers between devices with their start and end apart: 5, of which 4 were waited for; matrix products, arithmetic and copies ran while one was open for 3% of the time, Pallas kernels for 0%

commit v1 on v0

--- a/solution.py
+++ b/solution.py
@@ -11,6 +11,15 @@
 CAP = 2
 NORM_EPS = 1e-05
 STEP_EPS = 1e-06
+
+
+def added_up(value, name):
+    size = lax.axis_size(name)
+    summed, far = (value, 1)
+    while far < size:
+        summed = summed + lax.ppermute(summed, name, [(i, i ^ far) for i in range(size)])
+        far = 2 * far
+    return summed
 
 
 def expert_ffn(received, gate_proj, up_proj, down_proj):
@@ -56,7 +65,7 @@
         input_proj,
         preferred_element_type=jnp.float32,
     )
-    branch_full = lax.psum(branch_part, "state")
+    branch_full = added_up(branch_part, "state")
     conv_input = branch_full[0]
     gate_branch = branch_full[1]
     window = jnp.concatenate([conv_state, conv_input[None]], axis=0)

time: 227 us -> 201 us (0.89)
  waiting for transfers between devices: 78.8 us -> 56 us
  matrix products: 27.5 us -> 25.1 us
    psum x1 -> x0, waiting for transfers between devices: 27.6 us -> none  [per_device(): branch_full = lax.psum(branch_part, 'state')]
    ppermute x0 -> x2, waiting for transfers between devices: none -> 4.78 us  [added_up(): lax.ppermute(summed, name, [(i, i ^ far) for i in range(size)])]
    unnamed x4 -> x3, waiting for transfers between devices: 18.2 us -> 18.2 us
  transfers between devices with their start and end apart: 5 -> 6, of which waited for: 4 -> 5; matrix products, arithmetic and copies ran while one was open for 3% -> 3% of each run, Pallas kernels for 0% -> 0%
where the time goes in v1:
time: 201 us; the launch traced here: 200 us
  blocking collectives  77.1 us (38%)
  waiting for transfers between devices  56 us (28%)
  matrix products  25.1 us (12%)
  between operations  16.7 us (8%)
  other arithmetic  12 us (6%)
  starting transfers between devices  7.2 us (4%)
  local copies, waits for them, and re-layouts  5.8 us (3%)
    psum x1, waiting for transfers between devices, per_device(): readout = lax.psum(read_part, 'state')  27.5 us
    psum x1, blocking collectives, per_device(): projected = lax.psum(proj_part, 'head')  19 us
    unnamed x1, blocking collectives  19 us
    unnamed x3, waiting for transfers between devices  18.2 us
    all_gather x1, blocking collectives, per_device(): lax.all_gather(normed, 'head', axis=0, tiled=True)  13.4 us
    psum x1, blocking collectives, per_device(): load_sum, prob_sum = lax.psum((load_own, prob_own), 'head')  12.1 us
    psum x1, blocking collectives, per_device(): first_sq = lax.psum(jnp.sum(tok_f32 * tok_f32, axis=1), 'state')  8.36 us
    dot_general x1, matrix products, expert_ffn(): jnp.einsum('nlcd,ldf->nlcf', received, up_proj, preferred_element_type=jn...  7.47 us
  transfers between devices with their start and end apart: 6, of which 5 were waited for; matrix products, arithmetic and copies ran while one was open for 3% of the time, Pallas kernels for 0%

profile of v1, /device:TPU:0, one launch (start us, length us, event | category | flops | bytes accessed | tf_op | source)
XLA Modules:
  0.0 200.0 jit_solution(13717176801125133689)
XLA Ops:
  7.3 0.9 fusion.46
  8.2 8.4 %psum.35 = f32[4]{0:T(128)S(1)} all-reduce(f32[4]{0:T(128)S(1)} %fusion.46), channel_id=1, replica_groups=mesh['groups'=2,'head'=4,'state'=4] {'state'}, use_global_device_ids=true, to_apply=%region_1.0 | all-reduce | flops 4 | bytes 32 | tf_op jit(solution)/shard_map/psum | solution.py:59
  16.6 0.8 fusion.52
  17.4 13.4 %all-gather = bf16[4,4,512]{2,1,0:T(4,128)(2,1)S(1)} all-gather(bf16[1,4,512]{2,1,0:T(4,128)(2,1)S(1)} %fusion.52), channel_id=1, replica_groups=mesh['groups'=2,'head'=4,'state'=4] {'head'}, dimensions={0}, use_global_device_ids=true | all-gather | bytes 20480 | tf_op jit(solution)/shard_map/all_gather | solution.py:64
  30.8 2.8 %convolution_bitcast_fusion = f32[2,16,2048]{2,1,0:T(8,128)S(1)} fusion(bf16[16,512,1]{1,0,2:T(8,128)(2,1)S(1)} %reshape.86, bf16[2,512,2048]{2,1,0:T(8,128)(2,1)} %param.23), kind=kOutput, calls=%fused_computation.6 | convolution fusion | flops 67108864 | bytes 4472832 | tf_op jit(solution)/shard_map/td,kdc->ktc/dot_general | solution.py:62
  33.7 0.8 iota_compare_fusion
  34.4 0.7 iota_compare_fusion.1
  35.1 0.1 collective-permute-done
  35.3 0.6 collective-permute-start.1
  35.8 0.1 fusion.45
  35.9 0.8 exp.33
  36.7 1.2 dynamic-slice
  38.6 0.7 broadcast_compare_fusion
  39.3 4.7 %collective-permute-done.1 = f32[2,16,2048]{2,1,0:T(8,128)S(1)} collective-permute-done((f32[2,16,2048]{2,1,0:T(8,128)S(1)}, f32[2,16,2048]{2,1,0:T(8,128)S(1)}, u32[]{:S(2)}, u32[]{:S(2)}) %collective-permute-start.1) | collective-permute-done | bytes 262176 | tf_op jit(solution)/shard_map/ppermute | solution.py:20
  44.0 1.1 fusion.26
  45.1 0.7 divide_multiply_fusion
  45.8 1.7 fusion.31
  47.5 19.0 %psum.36 = f32[16,288]{1,0:T(8,128)S(1)} all-reduce(f32[16,288]{1,0:T(8,128)S(1)} %fusion.31), channel_id=1, replica_groups=mesh['groups'=2,'head'=4,'state'=4] {'head'}, use_global_device_ids=true, to_apply=%region_3.4 | all-reduce | flops 4608 | bytes 36864 | tf_op jit(solution)/shard_map/psum | solution.py:77
  66.5 0.1 multiply_reduce_fusion.1
  66.7 0.1 copy.53
  66.8 0.1 copy.54
  66.9 1.5 fusion.56
  68.4 2.7 %multiply_reduce_fusion = (f32[16,2048]{1,0:T(8,128)}, f32[4,16,2048]{2,1,0:T(8,128)}) fusion(f32[4,16]{1,0:T(4,128)S(1)} %copy.53, f32[16,2048]{1,0:T(8,128)S(1)} %divide_multiply_fusion, f32[4,16]{1,0:T(4,128)S(1)} %copy.54, f32[16,2048]{1,0:T(8,128)S(1)} %get-tuple-element.14, f32[4,16,2048]{2,1,0:T(8,128)} %param.33, f32[4,2048]{1,0:T(4,128)S(1)} %exp.33, ...), kind=kLoop, calls=%fused_computation.23 | loop fusion | flops 884736 | bytes 1606144 | tf_op jit(solution)/shard_map/reduce_sum | solution.py:91
  71.2 1.7 fusion.27
  72.9 27.5 %all-reduce.4.cloned.1.call-done = f32[16,2048]{1,0:T(8,128)} async-done(((f32[16,2048]{1,0:T(8,128)}), f32[16,2048]{1,0:T(8,128)}) %all-reduce.4.cloned.1.call-update) | async-done | bytes 131088 | tf_op jit(solution)/shard_map/psum | solution.py:92
  100.4 1.3 fusion.28
  101.7 19.0 %all-reduce = f32[16,512]{1,0:T(8,128)S(1)} all-reduce(f32[16,512]{1,0:T(8,128)S(1)} %fusion.28), channel_id=2, replica_groups=mesh['groups'=2,'head'=4,'state'=4] {'head'}, use_global_device_ids=true, to_apply=%region_7.8.clone | all-reduce | flops 8192 | bytes 65536
  120.7 5.2 %all_gather.7 = bf16[4,2048]{1,0:T(4,128)(2,1)S(1)} all-gather(bf16[4,512]{1,0:T(4,128)(2,1)S(1)} %fusion.49), channel_id=1, replica_groups=mesh['groups'=2,'head'=4,'state'=4] {'state'}, dimensions={1}, use_global_device_ids=true | all-gather | bytes 20480 | tf_op jit(solution)/shard_map/all_gather | solution.py:101
  125.9 0.1 fusion.38
  126.0 0.3 fusion.54
  126.3 0.2 convolution_convert_fusion
  126.5 0.7 copy.63
  127.2 3.3 %all-to-all-start = ((bf16[4,2,2,2048]{3,2,1,0:T(2,128)(2,1)}), bf16[4,2,2,2048]{3,2,1,0:T(2,128)(2,1)S(1)}, u32[]{:S(2)}, u32[]{:S(2)}) async-start(bf16[4,2,2,2048]{3,2,1,0:T(2,128)(2,1)} %bitcast.6), calls=%async_computation | async-start | bytes 131072 | tf_op jit(solution)/shard_map/all_to_all | solution.py:128
  130.5 0.2 select_reduce_fusion
  130.7 12.1 %all-reduce.1 = (f32[8]{0:T(128)S(1)}, f32[8]{0:T(128)S(1)}) all-reduce(f32[8]{0:T(128)S(1)} %get-tuple-element.5, f32[8]{0:T(128)S(1)} %get-tuple-element.15), channel_id=1, replica_groups=mesh['groups'=2,'head'=4,'state'=4] {'head'}, use_global_device_ids=true, to_apply=%region_14.15 | all-reduce | flops 16 | bytes 128 | tf_op jit(solution)/shard_map/psum | solution.py:149
  142.9 7.5 %fusion.6 = f32[4,2,2,1792]{3,0,2,1:T(4,128)S(1)} fusion(bf16[2,2048,1792]{2,1,0:T(8,128)(2,1)} %param.39, bf16[4,2,2,2048]{3,2,1,0:T(2,128)(2,1)S(1)} %all-to-all-done), kind=kOutput, calls=%fused_computation.7 | convolution fusion | flops 117440512 | bytes 14860288 | tf_op jit(solution)/shard_map/nlcd,ldf->nlcf/dot_general | solution.py:26
  150.4 7.5 %fusion.15 = bf16[4,2,2,1792]{3,0,2,1:T(4,128)(2,1)S(1)} fusion(bf16[2,2048,1792]{2,1,0:T(8,128)(2,1)} %param.40, f32[4,2,2,1792]{3,0,2,1:T(4,128)S(1)} %fusion.6, bf16[4,2,2,2048]{3,2,1,0:T(2,128)(2,1)S(1)} %all-to-all-done), kind=kOutput, calls=%fused_computation.11 | convolution fusion | flops 117612544 | bytes 14917632 | tf_op jit(solution)/shard_map/nlcd,ldf->nlcf/dot_general | solution.py:27
  157.9 2.1 %fusion.21 = bf16[4,2,2,2048]{3,0,2,1:T(4,128)(2,1)S(1)} fusion(bf16[4,2,2,1792]{3,0,2,1:T(4,128)(2,1)S(1)} %fusion.15, bf16[2,1792,2048]{2,1,0:T(8,128)(2,1)S(1)} %bitcast.72), kind=kOutput, calls=%fused_computation.14 | convolution fusion | flops 117473280 | bytes 14802944 | tf_op jit(solution)/shard_map/nlcf,lfd->nlcd/dot_general | solution.py:29
  160.0 0.7 copy.58
  160.7 3.3 %all-to-all-start.1 = ((bf16[4,2,2,2048]{3,2,1,0:T(2,128)(2,1)}), bf16[4,2,2,2048]{3,2,1,0:T(2,128)(2,1)S(1)}, u32[]{:S(2)}, u32[]{:S(2)}) async-start(bf16[4,2,2,2048]{3,2,1,0:T(2,128)(2,1)} %copy.58), calls=%async_computation.1 | async-start | bytes 131072 | tf_op jit(solution)/shard_map/all_to_all | solution.py:133
  164.1 0.1 fusion.44
  164.1 5.6 %all-to-all-done.1 = bf16[4,2,2,2048]{3,2,1,0:T(2,128)(2,1)S(1)} async-done(((bf16[4,2,2,2048]{3,2,1,0:T(2,128)(2,1)}), bf16[4,2,2,2048]{3,2,1,0:T(2,128)(2,1)S(1)}, u32[]{:S(2)}, u32[]{:S(2)}) %all-to-all-start.1) | async-done | bytes 65568 | tf_op jit(solution)/shard_map/all_to_all | solution.py:133
  169.7 0.2 fusion.24
  170.0 1.1 copy.64
  171.0 0.6 multiply_reduce_fusion.2
  172.3 18.1 %reduce-scatter.4.cloned.1.call-done = bf16[512,4]{1,0:T(8,128)(2,1)} async-done(((bf16[2048,4]{1,0:T(8,128)(2,1)}), bf16[512,4]{1,0:T(8,128)(2,1)}) %reduce-scatter.4.cloned.1.call-update) | async-done | bytes 4112
  190.4 1.0 copy.65
  191.4 0.6 add_convert_fusion
  (40 shorter events, 0.4 us)
Async XLA Ops:
  7.2 93.2 %copy-start = (bf16[2048,512]{1,0:T(8,128)(2,1)S(1)}, bf16[2048,512]{1,0:T(8,128)(2,1)}, u32[]{:S(2)}) copy-start(bf16[2048,512]{1,0:T(8,128)(2,1)} %param.34) | copy-start | bytes 6291460
  7.2 113.5 %copy-start.1 = (bf16[4,512]{1,0:T(4,128)(2,1)S(1)}, bf16[4,512]{1,0:T(4,128)(2,1)}, u32[]{:S(2)}) copy-start(bf16[4,512]{1,0:T(4,128)(2,1)} %param.21) | copy-start | bytes 12292
  7.2 123.3 %copy-start.3 = (s32[4,2]{0,1:T(2,128)S(1)}, s32[4,2]{0,1:T(2,128)}, u32[]{:S(2)}) copy-start(s32[4,2]{0,1:T(2,128)} %param.37) | copy-start | bytes 100
  7.2 123.5 %copy-start.4 = (s32[4,2]{0,1:T(2,128)S(1)}, s32[4,2]{0,1:T(2,128)}, u32[]{:S(2)}) copy-start(s32[4,2]{0,1:T(2,128)} %param.38) | copy-start | bytes 100
  7.2 118.8 %copy-start.2 = (f32[2048]{0:T(1024)S(1)}, f32[2048]{0:T(1024)}, u32[]{:S(2)}) copy-start(f32[2048]{0:T(1024)} %param.35) | copy-start | bytes 24580
  7.2 118.8 %copy-start.5 = (f32[2048,8]{0,1:T(8,128)S(1)}, f32[2048,8]{0,1:T(8,128)}, u32[]{:S(2)}) copy-start(f32[2048,8]{0,1:T(8,128)} %param.36) | copy-start | bytes 196612
  7.2 93.1 %all-reduce.4.cloned.1.call-start = ((), (), s32[]{:S(2)}) async-start(), calls=%async_computation.3 | async-start | bytes 262144 | tf_op jit(solution)/shard_map/psum | solution.py:92
  33.7 1.5 collective-permute-start
  35.3 8.7 %collective-permute-start.1 = (f32[2,16,2048]{2,1,0:T(8,128)S(1)}, f32[2,16,2048]{2,1,0:T(8,128)S(1)}, u32[]{:S(2)}, u32[]{:S(2)}) collective-permute-start(f32[2,16,2048]{2,1,0:T(8,128)S(1)} %add.107), channel_id=1, source_target_pairs={{0,2},{1,3},{2,0},{3,1},{4,6},{5,7},{6,4},{7,5},{8,10},{9,11},{10,... | collective-permute-start | bytes 786440 | tf_op jit(solution)/shard_map/ppermute | solution.py:20
  127.2 15.7 %all-to-all-start = ((bf16[4,2,2,2048]{3,2,1,0:T(2,128)(2,1)}), bf16[4,2,2,2048]{3,2,1,0:T(2,128)(2,1)S(1)}, u32[]{:S(2)}, u32[]{:S(2)}) async-start(bf16[4,2,2,2048]{3,2,1,0:T(2,128)(2,1)} %bitcast.6), calls=%async_computation | async-start | bytes 131072 | tf_op jit(solution)/shard_map/all_to_all | solution.py:128
  142.9 28.1 %copy-start.6 = (f32[8]{0:T(128)}, f32[8]{0:T(128)S(1)}, u32[]{:S(2)}) copy-start(f32[8]{0:T(128)S(1)} %get-tuple-element.7) | copy-start | bytes 100
  142.9 15.0 %slice-start = ((s8[14680064]{0:T(1024)(128)(4,1)}), s8[4194304]{0:T(1024)(128)(4,1)S(1)}, s32[]{:S(2)}) async-start(s8[14680064]{0:T(1024)(128)(4,1)} %bitcast.71), calls=%async_computation.5 | async-start | bytes 8388608
  142.9 15.0 %slice-start.1 = ((s8[14680064]{0:T(1024)(128)(4,1)}), s8[4194304]{0:T(1024)(128)(4,1)S(1)}, s32[]{:S(2)}) async-start(s8[14680064]{0:T(1024)(128)(4,1)} %bitcast.71), calls=%async_computation.6 | async-start | bytes 8388608
  150.4 7.5 %slice-start.2 = ((s8[14680064]{0:T(1024)(128)(4,1)}), s8[4194304]{0:T(1024)(128)(4,1)S(1)}, s32[]{:S(2)}) async-start(s8[14680064]{0:T(1024)(128)(4,1)} %bitcast.71), calls=%async_computation.7 | async-start | bytes 8388608
  150.4 7.5 %slice-start.3 = ((s8[14680064]{0:T(1024)(128)(4,1)}), s8[2097152]{0:T(1024)(128)(4,1)S(1)}, s32[]{:S(2)}) async-start(s8[14680064]{0:T(1024)(128)(4,1)} %bitcast.71), calls=%async_computation.8 | async-start | bytes 4194304
  160.7 9.0 %all-to-all-start.1 = ((bf16[4,2,2,2048]{3,2,1,0:T(2,128)(2,1)}), bf16[4,2,2,2048]{3,2,1,0:T(2,128)(2,1)S(1)}, u32[]{:S(2)}, u32[]{:S(2)}) async-start(bf16[4,2,2,2048]{3,2,1,0:T(2,128)(2,1)} %copy.58), calls=%async_computation.1 | async-start | bytes 131072 | tf_op jit(solution)/shard_map/all_to_all | solution.py:133
  164.0 26.4 %reduce-scatter.4.cloned.1.call-start = ((), (), s32[]{:S(2)}) async-start(), calls=%async_computation.4 | async-start | bytes 655360
Sparse Core Ops, SparseCore 0:
  71.3 29.0 all-reduce.3
  171.1 19.2 reduce-scatter.3
